TPU v7x, 256 devices: a whole 4x4x8 slice. The times are simulated.
256 devices in a mesh: vp: 64 (over y, z, core), rep: 4 (over x).
Axes of the slice: x: 4, y: 4, z: 8, core: 2. Of those that a mesh axis runs over, the one named last changes fastest.
Arguments:
- features: bfloat16 [524288, 256], P(('vp', 'rep')), may hold values from -48 to 48
- tile_values: bfloat16 [65536, 128, 128], P(('vp', 'rep')), may hold values from 0 to 0.0014648438
- tile_cols: int32 [65536], P(('vp', 'rep')), may hold values from 0 to 31, as said below
- halo_rows: int32 [256, 4, 4], P(('vp', 'rep')), may hold values from 0 to 15
Outputs:
- scores: bfloat16 [524288, 256], P(('vp', 'rep'))
Inputs may be any that keep to these rules, and one draw needn't show every extreme that they name: `tile_cols`: values below 16 name one of the shard's own row blocks; value 16 + o * 4 + j names the j-th block sent by peer o. Every value occurs on every shard.
All inputs are finite; a program needn't handle non-finite values.
Results may differ from a plain program's by a relative error of at most 0.002.
Values may be sent and summed in bfloat16 or wider, within the bound.
No kernel may reach another device: no remote copies, remote signals or barrier semaphores. Data moves between devices by JAX's collectives and lax.ppermute only.
A program may use at most 128 MiB of HBM per device.

v0:
```python
import jax
import jax.numpy as jnp
from jax import lax
from jax.sharding import PartitionSpec as P

ITERS = 3


peer_offsets = (1, -1, 4, -4)


def passed_along(shard, axis, by):
    count = lax.axis_size(axis)
    return lax.ppermute(shard, axis, [(i, (i + by) % count) for i in range(count)])


def total_of_pieces(shard, axis):
    blocks = lax.all_gather(shard, axis)
    return blocks.sum(axis=0)


def copy_for_each(shard, axis):
    count = lax.axis_size(axis)
    return lax.all_to_all(
        jnp.broadcast_to(shard[None], (count, *shard.shape)), axis, 0, 0, tiled=True
    )


def of_everyone(shard, axis):
    everything = copy_for_each(shard, axis)
    return jnp.sum(everything, axis=0)


def local(features, tile_values, tile_cols, halo_rows):
    tile_size = tile_values.shape[1]
    classes = features.shape[1]
    nblocks = features.shape[0] // tile_size
    per_row = tile_values.shape[0] // nblocks
    shards = lax.axis_size("vp") * lax.axis_size("rep")
    vertices = features.shape[0] * shards
    send_lists = halo_rows[0]
    tiles = tile_values.reshape(nblocks, per_row, tile_size, tile_size)
    tile_slots = tile_cols.reshape(nblocks, per_row)
    current = features
    for iteration in range(ITERS):
        own_blocks = current.reshape(nblocks, tile_size, classes)
        halo_blocks = []
        for which in range(4):
            halo_blocks.append(
                passed_along(own_blocks[send_lists[which]], ("vp", "rep"), peer_offsets[which])
            )
        block_table = jnp.concatenate([own_blocks] + halo_blocks, axis=0)
        picked = block_table[tile_slots]
        propagated = jnp.einsum(
            "rtij,rtjc->ric", tiles, picked, preferred_element_type=jnp.float32
        ).reshape(-1, classes)
        blended = 0.9 * propagated + 0.1 * features.astype(jnp.float32)
        local_mass = jnp.sum(blended * blended, axis=0)
        group_mass = total_of_pieces(local_mass, "rep")
        total_mass = of_everyone(group_mass, "vp")
        current = (blended / jnp.sqrt(0.05 + total_mass / vertices)).astype(jnp.bfloat16)
    return current


def solution(mesh):
    return jax.shard_map(
        local,
        mesh=mesh,
        in_specs=(
            P(("vp", "rep"), None),
            P(("vp", "rep"), None, None),
            P(("vp", "rep")),
            P(("vp", "rep"), None, None),
        ),
        out_specs=P(("vp", "rep"), None),
        check_vma=False,
    )
```

profile of v0, /device:TPU:32, one launch (start us, length us, event | category | flops | bytes accessed | tf_op | source)
XLA Modules:
  0.0 220.2 jit_solution(6301716887849608904)
XLA Ops:
  2.8 2.5 %gather_fusion.1 = bf16[4,128,256]{2,1,0:T(8,128)(2,1)} fusion(bf16[16,128,256]{2,1,0:T(8,128)(2,1)} %bitcast.74, s32[1024]{0:T(1024)S(1)} %pad_clamp_fusion.3), kind=kCustom, calls=%fused_computation.1 | custom fusion | bytes 524304 | tf_op jit(solution)/shard_map/gather | solution.py:50
  5.2 2.4 %collective-permute-start.1 = (bf16[4,128,256]{2,1,0:T(8,128)(2,1)}, bf16[4,128,256]{2,1,0:T(8,128)(2,1)}, u32[]{:S(2)}, u32[]{:S(2)}) collective-permute-start(bf16[4,128,256]{2,1,0:T(8,128)(2,1)} %gather_fusion.1), channel_id=1, source_target_pairs={{0,255},{1,0},{2,1},{3,2},{4,3},{5,4},{6,5},{7,6},{8,7},{9,8},{10,... | collective-permute-start | bytes 786440 | tf_op jit(solution)/shard_map/ppermute | solution.py:14
  7.6 2.5 %gather_fusion = bf16[4,128,256]{2,1,0:T(8,128)(2,1)} fusion(bf16[16,128,256]{2,1,0:T(8,128)(2,1)} %bitcast.75, s32[1024]{0:T(1024)S(1)} %pad_clamp_fusion.4), kind=kCustom, calls=%fused_computation | custom fusion | bytes 524304 | tf_op jit(solution)/shard_map/gather | solution.py:50
  10.1 2.5 %gather_fusion.2 = bf16[4,128,256]{2,1,0:T(8,128)(2,1)} fusion(bf16[16,128,256]{2,1,0:T(8,128)(2,1)} %bitcast.76, s32[1024]{0:T(1024)S(1)} %pad_clamp_fusion.2), kind=kCustom, calls=%fused_computation.2 | custom fusion | bytes 524304 | tf_op jit(solution)/shard_map/gather | solution.py:50
  13.4 5.0 %collective-permute-done = bf16[4,128,256]{2,1,0:T(8,128)(2,1)} collective-permute-done((bf16[4,128,256]{2,1,0:T(8,128)(2,1)}, bf16[4,128,256]{2,1,0:T(8,128)(2,1)}, u32[]{:S(2)}, u32[]{:S(2)}) %collective-permute-start) | collective-permute-done | bytes 262176 | tf_op jit(solution)/shard_map/ppermute | solution.py:14
  20.4 4.5 %collective-permute-done.2 = bf16[4,128,256]{2,1,0:T(8,128)(2,1)} collective-permute-done((bf16[4,128,256]{2,1,0:T(8,128)(2,1)}, bf16[4,128,256]{2,1,0:T(8,128)(2,1)}, u32[]{:S(2)}, u32[]{:S(2)}) %collective-permute-start.2) | collective-permute-done | bytes 262176 | tf_op jit(solution)/shard_map/ppermute | solution.py:14
  26.9 9.7 %gather_fusion.4 = bf16[256,128,256]{2,1,0:T(8,128)(2,1)} fusion(bf16[32,128,256]{2,1,0:T(8,128)(2,1)S(1)} %constant_dynamic-update-slice_fusion, s32[1024]{0:T(1024)S(1)} %pad_clamp_fusion), kind=kCustom, calls=%fused_computation.4 | custom fusion | bytes 33555456 | tf_op jit(solution)/shard_map/gather | solution.py:53
  36.6 10.5 %bitcast_multiply_fusion.2 = f32[16,256,128]{1,2,0:T(8,128)S(1)} fusion(bf16[16,16,128,128]{3,2,1,0:T(8,128)(2,1)} %bitcast.67, bf16[16,16,128,256]{3,2,1,0:T(8,128)(2,1)} %bitcast.71), kind=kOutput, calls=%fused_computation.20 | convolution fusion | flops 2148007936 | bytes 27262976 | tf_op jit(solution)/shard_map/rtij,rtjc->ric/dot_general | solution.py:54
  47.6 7.0 %all-gather.3 = f32[4,1,256]{2,1,0:T(1,128)S(1)} all-gather(f32[1,1,256]{2,1,0:T(1,128)S(1)} %bitcast.88), channel_id=2, replica_groups=mesh['vp'=64,'rep'=4] {'rep'}, dimensions={0}, use_global_device_ids=true | all-gather | bytes 5120 | tf_op jit(solution)/shard_map/all_gather | solution.py:18
  54.6 21.6 %all_to_all.18 = f32[64,1,256]{2,1,0:T(1,128)S(1)} all-to-all(f32[64,1,256]{2,1,0:T(1,128)S(1)} %broadcast_in_dim.6), channel_id=1, replica_groups=mesh['vp'=64,'rep'=4] {'vp'}, dimensions={0} | all-to-all | bytes 131072 | tf_op jit(solution)/shard_map/all_to_all | solution.py:24
  77.6 2.5 %gather_fusion.5 = bf16[4,128,256]{2,1,0:T(8,128)(2,1)} fusion(bf16[16,128,256]{2,1,0:T(8,128)(2,1)} %bitcast.83, s32[1024]{0:T(1024)S(1)} %pad_clamp_fusion.4), kind=kCustom, calls=%fused_computation.5 | custom fusion | bytes 524304 | tf_op jit(solution)/shard_map/gather | solution.py:50
  82.1 2.5 %gather_fusion.6 = bf16[4,128,256]{2,1,0:T(8,128)(2,1)} fusion(bf16[16,128,256]{2,1,0:T(8,128)(2,1)} %bitcast.84, s32[1024]{0:T(1024)S(1)} %pad_clamp_fusion.3), kind=kCustom, calls=%fused_computation.6 | custom fusion | bytes 524304 | tf_op jit(solution)/shard_map/gather | solution.py:50
  86.5 2.5 %gather_fusion.7 = bf16[4,128,256]{2,1,0:T(8,128)(2,1)} fusion(bf16[16,128,256]{2,1,0:T(8,128)(2,1)} %bitcast.85, s32[1024]{0:T(1024)S(1)} %pad_clamp_fusion.2), kind=kCustom, calls=%fused_computation.7 | custom fusion | bytes 524304 | tf_op jit(solution)/shard_map/gather | solution.py:50
  97.8 9.7 %gather_fusion.9 = bf16[256,128,256]{2,1,0:T(8,128)(2,1)} fusion(bf16[32,128,256]{2,1,0:T(8,128)(2,1)S(1)} %constant_dynamic-update-slice_fusion.5, s32[1024]{0:T(1024)S(1)} %pad_clamp_fusion), kind=kCustom, calls=%fused_computation.9 | custom fusion | bytes 33555456 | tf_op jit(solution)/shard_map/gather | solution.py:53
  107.5 10.5 %bitcast_multiply_fusion.1 = f32[16,256,128]{1,2,0:T(8,128)S(1)} fusion(bf16[16,16,128,128]{3,2,1,0:T(8,128)(2,1)} %bitcast.68, bf16[16,16,128,256]{3,2,1,0:T(8,128)(2,1)} %bitcast.72), kind=kOutput, calls=%fused_computation.19 | convolution fusion | flops 2148007936 | bytes 27262976 | tf_op jit(solution)/shard_map/rtij,rtjc->ric/dot_general | solution.py:54
  118.5 7.2 %all-gather.4 = f32[4,1,256]{2,1,0:T(1,128)S(1)} all-gather(f32[1,1,256]{2,1,0:T(1,128)S(1)} %bitcast.89), channel_id=3, replica_groups=mesh['vp'=64,'rep'=4] {'rep'}, dimensions={0}, use_global_device_ids=true | all-gather | bytes 5120 | tf_op jit(solution)/shard_map/all_gather | solution.py:18
  125.7 21.8 %all_to_all.19 = f32[64,1,256]{2,1,0:T(1,128)S(1)} all-to-all(f32[64,1,256]{2,1,0:T(1,128)S(1)} %broadcast_in_dim.7), channel_id=1, replica_groups=mesh['vp'=64,'rep'=4] {'vp'}, dimensions={0} | all-to-all | bytes 131072 | tf_op jit(solution)/shard_map/all_to_all | solution.py:24
  148.8 2.5 %gather_fusion.10 = bf16[4,128,256]{2,1,0:T(8,128)(2,1)} fusion(bf16[16,128,256]{2,1,0:T(8,128)(2,1)} %bitcast.78, s32[1024]{0:T(1024)S(1)} %pad_clamp_fusion.4), kind=kCustom, calls=%fused_computation.10 | custom fusion | bytes 524304 | tf_op jit(solution)/shard_map/gather | solution.py:50
  153.0 2.5 %gather_fusion.11 = bf16[4,128,256]{2,1,0:T(8,128)(2,1)} fusion(bf16[16,128,256]{2,1,0:T(8,128)(2,1)} %bitcast.79, s32[1024]{0:T(1024)S(1)} %pad_clamp_fusion.3), kind=kCustom, calls=%fused_computation.11 | custom fusion | bytes 524304 | tf_op jit(solution)/shard_map/gather | solution.py:50
  160.8 2.5 %gather_fusion.13 = bf16[4,128,256]{2,1,0:T(8,128)(2,1)} fusion(bf16[16,128,256]{2,1,0:T(8,128)(2,1)} %bitcast.82, s32[1024]{0:T(1024)S(1)} %pad_clamp_fusion.1), kind=kCustom, calls=%fused_computation.13 | custom fusion | bytes 524304 | tf_op jit(solution)/shard_map/gather | solution.py:50
  169.3 9.7 %gather_fusion.14 = bf16[256,128,256]{2,1,0:T(8,128)(2,1)} fusion(bf16[32,128,256]{2,1,0:T(8,128)(2,1)S(1)} %constant_dynamic-update-slice_fusion.10, s32[1024]{0:T(1024)S(1)} %pad_clamp_fusion), kind=kCustom, calls=%fused_computation.14 | custom fusion | bytes 33555456 | tf_op jit(solution)/shard_map/gather | solution.py:53
  179.0 10.5 %bitcast_multiply_fusion = f32[16,256,128]{1,2,0:T(8,128)S(1)} fusion(bf16[16,16,128,128]{3,2,1,0:T(8,128)(2,1)} %bitcast.69, bf16[16,16,128,256]{3,2,1,0:T(8,128)(2,1)} %bitcast.70), kind=kOutput, calls=%fused_computation.18 | convolution fusion | flops 2148007936 | bytes 27262976 | tf_op jit(solution)/shard_map/rtij,rtjc->ric/dot_general | solution.py:54
  190.0 7.0 %all-gather.5 = f32[4,1,256]{2,1,0:T(1,128)S(1)} all-gather(f32[1,1,256]{2,1,0:T(1,128)S(1)} %bitcast.90), channel_id=4, replica_groups=mesh['vp'=64,'rep'=4] {'rep'}, dimensions={0}, use_global_device_ids=true | all-gather | bytes 5120 | tf_op jit(solution)/shard_map/all_gather | solution.py:18
  197.0 21.8 %all_to_all.20 = f32[64,1,256]{2,1,0:T(1,128)S(1)} all-to-all(f32[64,1,256]{2,1,0:T(1,128)S(1)} %broadcast_in_dim.8), channel_id=1, replica_groups=mesh['vp'=64,'rep'=4] {'vp'}, dimensions={0} | all-to-all | bytes 131072 | tf_op jit(solution)/shard_map/all_to_all | solution.py:24
  (70 shorter events, 38.6 us)
Async XLA Ops:
  0.0 13.2 %copy-start = (bf16[2048,256]{1,0:T(8,128)(2,1)S(1)}, bf16[2048,256]{1,0:T(8,128)(2,1)}, u32[]{:S(2)}) copy-start(bf16[2048,256]{1,0:T(8,128)(2,1)} %param.4) | copy-start | bytes 3145732
  0.0 13.1 %copy-start.1 = (s32[256]{0:T(256)S(1)}, s32[256]{0:T(256)}, u32[]{:S(2)}) copy-start(s32[256]{0:T(256)} %param.6) | copy-start | bytes 3076
  2.6 23.3 %collective-permute-start.3 = (bf16[4,128,256]{2,1,0:T(8,128)(2,1)S(1)}, bf16[4,128,256]{2,1,0:T(8,128)(2,1)}, u32[]{:S(2)}, u32[]{:S(2)}) collective-permute-start(bf16[4,128,256]{2,1,0:T(8,128)(2,1)S(1)} %gather_fusion.3), channel_id=1, source_target_pairs={{0,252},{1,253},{2,254},{3,255},{4,0},{5,1},{6,2},{7,3},{8,4},{9,5... | collective-permute-start | bytes 786440 | tf_op jit(solution)/shard_map/ppermute | solution.py:14
  5.2 14.2 %collective-permute-start.1 = (bf16[4,128,256]{2,1,0:T(8,128)(2,1)}, bf16[4,128,256]{2,1,0:T(8,128)(2,1)}, u32[]{:S(2)}, u32[]{:S(2)}) collective-permute-start(bf16[4,128,256]{2,1,0:T(8,128)(2,1)} %gather_fusion.1), channel_id=1, source_target_pairs={{0,255},{1,0},{2,1},{3,2},{4,3},{5,4},{6,5},{7,6},{8,7},{9,8},{10,... | collective-permute-start | bytes 786440 | tf_op jit(solution)/shard_map/ppermute | solution.py:14
  10.1 8.3 %collective-permute-start = (bf16[4,128,256]{2,1,0:T(8,128)(2,1)}, bf16[4,128,256]{2,1,0:T(8,128)(2,1)}, u32[]{:S(2)}, u32[]{:S(2)}) collective-permute-start(bf16[4,128,256]{2,1,0:T(8,128)(2,1)} %gather_fusion), channel_id=1, source_target_pairs={{0,1},{1,2},{2,3},{3,4},{4,5},{5,6},{6,7},{7,8},{8,9},{9,10},{10,1... | collective-permute-start | bytes 786440 | tf_op jit(solution)/shard_map/ppermute | solution.py:14
  12.6 12.3 %collective-permute-start.2 = (bf16[4,128,256]{2,1,0:T(8,128)(2,1)}, bf16[4,128,256]{2,1,0:T(8,128)(2,1)}, u32[]{:S(2)}, u32[]{:S(2)}) collective-permute-start(bf16[4,128,256]{2,1,0:T(8,128)(2,1)} %gather_fusion.2), channel_id=1, source_target_pairs={{0,4},{1,5},{2,6},{3,7},{4,8},{5,9},{6,10},{7,11},{8,12},{9,13},{1... | collective-permute-start | bytes 786440 | tf_op jit(solution)/shard_map/ppermute | solution.py:14
  80.1 13.8 %collective-permute-start.4 = (bf16[4,128,256]{2,1,0:T(8,128)(2,1)}, bf16[4,128,256]{2,1,0:T(8,128)(2,1)}, u32[]{:S(2)}, u32[]{:S(2)}) collective-permute-start(bf16[4,128,256]{2,1,0:T(8,128)(2,1)} %gather_fusion.5), channel_id=1, source_target_pairs={{0,1},{1,2},{2,3},{3,4},{4,5},{5,6},{6,7},{7,8},{8,9},{9,10},{10,1... | collective-permute-start | bytes 786440 | tf_op jit(solution)/shard_map/ppermute | solution.py:14
  84.6 10.2 %collective-permute-start.5 = (bf16[4,128,256]{2,1,0:T(8,128)(2,1)}, bf16[4,128,256]{2,1,0:T(8,128)(2,1)}, u32[]{:S(2)}, u32[]{:S(2)}) collective-permute-start(bf16[4,128,256]{2,1,0:T(8,128)(2,1)} %gather_fusion.6), channel_id=1, source_target_pairs={{0,255},{1,0},{2,1},{3,2},{4,3},{5,4},{6,5},{7,6},{8,7},{9,8},{10,... | collective-permute-start | bytes 786440 | tf_op jit(solution)/shard_map/ppermute | solution.py:14
  89.0 6.9 %collective-permute-start.6 = (bf16[4,128,256]{2,1,0:T(8,128)(2,1)}, bf16[4,128,256]{2,1,0:T(8,128)(2,1)}, u32[]{:S(2)}, u32[]{:S(2)}) collective-permute-start(bf16[4,128,256]{2,1,0:T(8,128)(2,1)} %gather_fusion.7), channel_id=1, source_target_pairs={{0,4},{1,5},{2,6},{3,7},{4,8},{5,9},{6,10},{7,11},{8,12},{9,13},{1... | collective-permute-start | bytes 786440 | tf_op jit(solution)/shard_map/ppermute | solution.py:14
  92.1 5.7 %collective-permute-start.7 = (bf16[4,128,256]{2,1,0:T(8,128)(2,1)S(1)}, bf16[4,128,256]{2,1,0:T(8,128)(2,1)S(1)}, u32[]{:S(2)}, u32[]{:S(2)}) collective-permute-start(bf16[4,128,256]{2,1,0:T(8,128)(2,1)S(1)} %gather_fusion.8), channel_id=1, source_target_pairs={{0,252},{1,253},{2,254},{3,255},{4,0},{5,1},{6,2},{7,3},{8,4},{9,5... | collective-permute-start | bytes 786440 | tf_op jit(solution)/shard_map/ppermute | solution.py:14
  151.3 13.8 %collective-permute-start.8 = (bf16[4,128,256]{2,1,0:T(8,128)(2,1)}, bf16[4,128,256]{2,1,0:T(8,128)(2,1)}, u32[]{:S(2)}, u32[]{:S(2)}) collective-permute-start(bf16[4,128,256]{2,1,0:T(8,128)(2,1)} %gather_fusion.10), channel_id=1, source_target_pairs={{0,1},{1,2},{2,3},{3,4},{4,5},{5,6},{6,7},{7,8},{8,9},{9,10},{10,1... | collective-permute-start | bytes 786440 | tf_op jit(solution)/shard_map/ppermute | solution.py:14
  155.5 10.5 %collective-permute-start.9 = (bf16[4,128,256]{2,1,0:T(8,128)(2,1)}, bf16[4,128,256]{2,1,0:T(8,128)(2,1)}, u32[]{:S(2)}, u32[]{:S(2)}) collective-permute-start(bf16[4,128,256]{2,1,0:T(8,128)(2,1)} %gather_fusion.11), channel_id=1, source_target_pairs={{0,255},{1,0},{2,1},{3,2},{4,3},{5,4},{6,5},{7,6},{8,7},{9,8},{10,... | collective-permute-start | bytes 786440 | tf_op jit(solution)/shard_map/ppermute | solution.py:14
  159.5 7.6 %collective-permute-start.10 = (bf16[4,128,256]{2,1,0:T(8,128)(2,1)S(1)}, bf16[4,128,256]{2,1,0:T(8,128)(2,1)}, u32[]{:S(2)}, u32[]{:S(2)}) collective-permute-start(bf16[4,128,256]{2,1,0:T(8,128)(2,1)S(1)} %gather_fusion.12), channel_id=1, source_target_pairs={{0,4},{1,5},{2,6},{3,7},{4,8},{5,9},{6,10},{7,11},{8,12},{9,13},{1... | collective-permute-start | bytes 786440 | tf_op jit(solution)/shard_map/ppermute | solution.py:14
  163.3 5.9 %collective-permute-start.11 = (bf16[4,128,256]{2,1,0:T(8,128)(2,1)}, bf16[4,128,256]{2,1,0:T(8,128)(2,1)S(1)}, u32[]{:S(2)}, u32[]{:S(2)}) collective-permute-start(bf16[4,128,256]{2,1,0:T(8,128)(2,1)} %gather_fusion.13), channel_id=1, source_target_pairs={{0,252},{1,253},{2,254},{3,255},{4,0},{5,1},{6,2},{7,3},{8,4},{9,5... | collective-permute-start | bytes 786440 | tf_op jit(solution)/shard_map/ppermute | solution.py:14
where the time goes:
time: 224 us; the launch traced here: 220 us
  blocking collectives  86.3 us (39%)
  local copies, waits for them, and re-layouts  69.7 us (31%)
  matrix products  31.5 us (14%)
  starting transfers between devices  14.3 us (6%)
  waiting for transfers between devices  11.8 us (5%)
  other arithmetic  6.41 us (3%)
    all_to_all x3, blocking collectives, copy_for_each(): lax.all_to_all(jnp.broadcast_to(shard[None], (count, *shard.shape)), axis...  65.2 us
    dot_general x3, matrix products, local(): jnp.einsum('rtij,rtjc->ric', tiles, picked, preferred_element_type=jnp.fl...  31.5 us
    gather x3, local copies, waits for them, and re-layouts, local(): picked = block_table[tile_slots]  29.2 us
    gather x12, local copies, waits for them, and re-layouts, local(): own_blocks[send_lists[which]]  27.8 us
    all_gather x3, blocking collectives, total_of_pieces(): blocks = lax.all_gather(shard, axis)  21.1 us
    ppermute x12, starting transfers between devices, passed_along(): lax.ppermute(shard, axis, [(i, (i + by) % count) for i in range(count)])  14.3 us
    ppermute x12, waiting for transfers between devices, passed_along(): lax.ppermute(shard, axis, [(i, (i + by) % count) for i in range(count)])  11.8 us
    unnamed x16, local copies, waits for them, and re-layouts  11.4 us
  transfers between devices with their start and end apart: 12, of which 4 were waited for; matrix products, arithmetic and copies ran while one was open for 15% of the time, Pallas kernels for 0%

commit v1 on v0

v1 whole, which is shorter than its diff:
```python
import functools

import jax
import jax.numpy as jnp
from jax import lax
from jax.experimental import pallas as pl
from jax.experimental.pallas import tpu as pltpu
from jax.sharding import Mesh
from jax.sharding import PartitionSpec as P

ALL = ("y", "z", "c", "x")
LIMIT = 4 * 1024 * 1024
TILE = 128
ROWS_PER_STEP = 4

VMEM = pl.BlockSpec(memory_space=pltpu.VMEM)
SMEM = pl.BlockSpec(memory_space=pltpu.SMEM)
HBM = pl.BlockSpec(memory_space=pltpu.HBM)
PARAMS = pltpu.CompilerParams(vmem_limit_bytes=LIMIT)


def parities():
    return lax.axis_index("x") % 2, lax.axis_index("c")


def send_lists():
    p, q = parities()
    return ((p, 1 - p), (1 - p, p), (2 + q, 3 - q), (3 - q, 2 + q))


def pairings(count):
    near = [(i, i ^ 1) for i in range(count)]
    near_odd = [(i, (i + 1) % count if i % 2 else (i - 1) % count) for i in range(count)]
    far = [(i, i ^ 4) for i in range(count)]
    far_odd = [(i, (i + 4) % count if (i // 4) % 2 else (i - 4) % count) for i in range(count)]
    return near, near_odd, far, far_odd


def pack(halo, table, sends):
    for (to, _), send in zip(send_lists(), sends):
        for j in range(send.shape[0]):
            send[j] = table[halo[0, to, j]]


def first_kernel(halo, features, *sends_and_sems):
    *sends, sems = sends_and_sems
    copies = []
    for k, (to, _) in enumerate(send_lists()):
        for j in range(sends[k].shape[0]):
            copies.append(
                pltpu.make_async_copy(features.at[halo[0, to, j]], sends[k].at[j], sems.at[k, j])
            )
            copies[-1].start()
    for copy in copies:
        copy.wait()


def load_kernel(features, tiles, table, kept, sems):
    copies = [
        pltpu.make_async_copy(features, table.at[pl.ds(0, features.shape[0])], sems.at[0]),
        pltpu.make_async_copy(tiles, kept, sems.at[1]),
    ]
    for copy in copies:
        copy.start()
    for copy in copies:
        copy.wait()


def fold(rows):
    return jnp.sum(rows.reshape(rows.shape[0] // 8, 8, rows.shape[1]), axis=0)


def gather_halo(table, received, nblocks):
    for (_, source), block in zip(send_lists(), received):
        size = block.shape[0]
        table[pl.ds(nblocks + source * size, size)] = block[...]


def row_product(row, per_row, cols, tiles, table):
    acc = None
    for t in range(0, per_row, 2):
        at = row * per_row + t
        left = jnp.concatenate([tiles[at], tiles[at + 1]], axis=1)
        right = jnp.concatenate([table[cols[at]], table[cols[at + 1]]], axis=0)
        part = jnp.dot(left, right, preferred_element_type=jnp.float32)
        acc = part if acc is None else acc + part
    return acc


def over_rows(nblocks, count, body):
    def step(i, sums):
        for k in range(ROWS_PER_STEP):
            sums = body(i * ROWS_PER_STEP + k, sums)
        return sums

    zero = tuple(jnp.zeros((8, 256), jnp.float32) for _ in range(count))
    return lax.fori_loop(0, nblocks // ROWS_PER_STEP, step, zero)


def write_sums(out, sums):
    for k, s in enumerate(sums):
        out[pl.ds(k, 1), :] = jnp.sum(s, axis=0, keepdims=True)


def step1_kernel(cols, halo, tiles, _, ra, rb, rc, rd, table, table_out, held, sums_out, *sends):
    nblocks = held.shape[0]
    per_row = tiles.shape[0] // nblocks
    gather_halo(table, (ra, rb, rc, rd), nblocks)

    def body(row, sums):
        spread = row_product(row, per_row, cols, tiles, table)
        held[row] = spread
        start = table[row].astype(jnp.float32)
        table_out[row] = (0.9 * spread + 0.1 * start).astype(jnp.bfloat16)
        new = (start * start, spread * start, spread * spread)
        return tuple(s + fold(n) for s, n in zip(sums, new))

    write_sums(sums_out, over_rows(nblocks, 3, body))
    pack(halo, table_out, sends)


def step2_kernel(cols, halo, tiles, features, _, ra, rb, rc, rd, table, table_out, sums_out, *sends):
    nblocks = features.shape[0] // 2
    per_row = tiles.shape[0] // nblocks
    gather_halo(table, (ra, rb, rc, rd), nblocks)

    def body(row, sums):
        spread = row_product(row, per_row, cols, tiles, table)
        start = features[row].astype(jnp.float32)
        table_out[row] = spread.astype(jnp.bfloat16)
        new = (spread * spread, spread * start)
        return tuple(s + fold(n) for s, n in zip(sums, new))

    write_sums(sums_out, over_rows(nblocks, 2, body))
    pack(halo, table_out, sends)


def step3_kernel(cols, tiles, features, held, _, ra, rb, rc, rd, table, spread_out, sums_out):
    nblocks = held.shape[0]
    per_row = tiles.shape[0] // nblocks
    gather_halo(table, (ra, rb, rc, rd), nblocks)

    def body(row, sums):
        spread = row_product(row, per_row, cols, tiles, table)
        spread_out[row] = spread
        start = features[row].astype(jnp.float32)
        new = (spread * spread, spread * start, spread * held[row])
        return tuple(s + fold(n) for s, n in zip(sums, new))

    write_sums(sums_out, over_rows(nblocks, 3, body))


def last_kernel(vertices, sums, features, held, spread, out):
    total = jnp.sum(sums[...], axis=0)
    ff, yf, yy, ww, wf, vv, vf, vy = [total[k : k + 1] for k in range(8)]

    def scale(mass):
        return 1.0 / jnp.sqrt(0.05 + mass * (1.0 / vertices))

    s1 = scale(0.81 * yy + 0.18 * yf + 0.01 * ff)
    s2 = scale(0.81 * s1 * s1 * ww + 0.18 * s1 * wf + 0.01 * ff)
    inner = 0.81 * s1 * s1 * vv + 0.18 * s1 * vy + 0.01 * yy
    cross = 0.9 * s1 * vf + 0.1 * yf
    s3 = scale(0.81 * s2 * s2 * inner + 0.18 * s2 * cross + 0.01 * ff)
    a = 0.81 * s1 * s2 * s3
    b = 0.09 * s2 * s3
    c = 0.1 * s3

    def body(row, carry):
        start = features[row].astype(jnp.float32)
        out[row] = (a * spread[row] + b * held[row] + c * start).astype(jnp.bfloat16)
        return carry

    lax.fori_loop(0, out.shape[0], body, 0)


def in_hbm(array):
    return pltpu.with_memory_space_constraint(array, pltpu.HBM)


def exchange(sends):
    perms = pairings(lax.axis_size(ALL))
    return [lax.ppermute(s, ALL, p) for s, p in zip(sends, perms)]


def join_kernel(first, second, third, out):
    joined = jnp.concatenate([first[...], second[...], third[...]], axis=0)
    out[...] = jnp.broadcast_to(joined[None], out.shape)


def add_kernel(sums, out):
    out[...] = jnp.broadcast_to(jnp.sum(sums[...], axis=0)[None], out.shape)


def spread_sums(kernel, axes, *sums):
    count = lax.axis_size(axes)
    copies = pl.pallas_call(
        kernel,
        out_shape=pltpu.VMEM((count, 8, sums[0].shape[-1]), jnp.float32),
        in_specs=[VMEM] * len(sums),
        out_specs=VMEM,
        compiler_params=PARAMS,
        name="copies",
    )(*sums)
    return lax.all_to_all(copies, axes, 0, 0, tiled=True)


def local(features, tile_values, tile_cols, halo_rows):
    tile = tile_values.shape[1]
    classes = features.shape[1]
    nblocks = features.shape[0] // tile
    peers, slots = halo_rows.shape[1:]
    vertices = features.shape[0] * lax.axis_size(ALL)
    blocks = in_hbm(features.reshape(nblocks, tile, classes))
    halo_rows = in_hbm(halo_rows)
    tile_cols = in_hbm(tile_cols)
    table_shape = pltpu.VMEM((nblocks + peers * slots, tile, classes), jnp.bfloat16)
    send_shape = [pltpu.VMEM((slots, tile, classes), jnp.bfloat16)] * peers
    wide = pltpu.VMEM((nblocks, tile, classes), jnp.float32)

    def sums_shape(count):
        return pltpu.VMEM((count, classes), jnp.float32)

    sends = pl.pallas_call(
        first_kernel,
        out_shape=send_shape,
        in_specs=[SMEM, HBM],
        out_specs=[VMEM] * 4,
        scratch_shapes=[pltpu.SemaphoreType.DMA((peers, slots))],
        compiler_params=PARAMS,
        name="first",
    )(halo_rows, blocks)
    received = exchange(sends)
    table0, kept = pl.pallas_call(
        load_kernel,
        out_shape=[table_shape, pltpu.VMEM(tile_values.shape, tile_values.dtype)],
        in_specs=[HBM, HBM],
        out_specs=[VMEM, VMEM],
        scratch_shapes=[pltpu.SemaphoreType.DMA((2,))],
        compiler_params=PARAMS,
        name="load",
    )(blocks, in_hbm(tile_values))
    table0, table1, held, sums1, *sends = pl.pallas_call(
        step1_kernel,
        out_shape=[table_shape, table_shape, wide, sums_shape(3)] + send_shape,
        input_output_aliases={3: 0},
        in_specs=[SMEM, SMEM] + [VMEM] * 6,
        out_specs=[VMEM] * 8,
        compiler_params=PARAMS,
        name="step1",
    )(tile_cols, halo_rows, kept, table0, *received)
    received = exchange(sends)
    _, table2, sums2, *sends = pl.pallas_call(
        step2_kernel,
        out_shape=[table_shape, table_shape, sums_shape(2)] + send_shape,
        input_output_aliases={4: 0},
        in_specs=[SMEM, SMEM] + [VMEM] * 7,
        out_specs=[VMEM] * 7,
        compiler_params=PARAMS,
        name="step2",
    )(tile_cols, halo_rows, kept, table0, table1, *received)
    received = exchange(sends)
    _, spread, sums3 = pl.pallas_call(
        step3_kernel,
        out_shape=[table_shape, wide, sums_shape(3)],
        input_output_aliases={4: 0},
        in_specs=[SMEM] + [VMEM] * 8,
        out_specs=[VMEM] * 3,
        compiler_params=PARAMS,
        name="step3",
    )(tile_cols, kept, table0, held, table2, *received)
    sums = spread_sums(join_kernel, ("c", "x"), sums1, sums2, sums3)
    sums = spread_sums(add_kernel, ("y", "z"), sums)
    out = pl.pallas_call(
        functools.partial(last_kernel, vertices),
        out_shape=jax.ShapeDtypeStruct((nblocks, tile, classes), jnp.bfloat16),
        in_specs=[VMEM] * 4,
        out_specs=VMEM,
        compiler_params=PARAMS,
        name="last",
    )(sums, table0, held, spread)
    return out.reshape(features.shape)


def solution(mesh):
    groups, reps = mesh.devices.shape
    grid = Mesh(mesh.devices.reshape(4, groups // 8, 2, reps), ALL)
    return jax.shard_map(
        local,
        mesh=grid,
        in_specs=(P(ALL, None), P(ALL, None, None), P(ALL), P(ALL, None, None)),
        out_specs=P(ALL, None),
        check_vma=False,
    )
```

time: 224 us -> 89.6 us (0.40); the launches traced: 220 us -> 89.3 us
  local copies, waits for them, and re-layouts: 69.7 us -> 0 us
  blocking collectives: 86.3 us -> 30.6 us
  matrix products: 31.5 us -> 0 us
  Pallas kernels: 0 us -> 20 us
  starting transfers between devices: 14.3 us -> 30.2 us
  other arithmetic: 6.41 us -> 0 us
  waiting for transfers between devices: 11.8 us -> 8.39 us
    gather x15 -> x0, local copies, waits for them, and re-layouts: 57 us -> none  [the longest x3 29.2 us: local(): picked = block_table[tile_slots]]
    all_to_all x3 -> x2, blocking collectives: 65.2 us -> 30.6 us  [spread_sums(): return lax.all_to_all(copies, axes, 0, 0, tiled=True)]
    dot_general x3 -> x0, matrix products: 31.5 us -> none  [local(): jnp.einsum('rtij,rtjc->ric', tiles, picked, preferred_element_type=jnp.fl...]
    all_gather x3 -> x0, blocking collectives: 21.1 us -> none  [total_of_pieces(): blocks = lax.all_gather(shard, axis)]
    pallas_call x0 -> x8, Pallas kernels: none -> 20 us  [the longest x1 4.14 us: local(): pl.pallas_call(step2_kernel, out_shape=[table_shape, table_shape, sums_sh...]
    ppermute x12, starting transfers between devices: 14.3 us -> 30.2 us  [exchange(): return [lax.ppermute(s, ALL, p) for s, p in zip(sends, perms)]]
    unnamed x16 -> x0, local copies, waits for them, and re-layouts: 11.4 us -> none
    convert_element_type x3 -> x0, other arithmetic: 3.89 us -> none  [local(): (blended / jnp.sqrt(0.05 + total_mass / vertices)).astype(jnp.bfloat16)]
  transfers between devices with their start and end apart: 12 -> 12, of which waited for: 4 -> 3; matrix products, arithmetic and copies ran while one was open for 15% -> 0% of each run, Pallas kernels for 0% -> 4%
where the time goes in v1:
time: 89.6 us; the launch traced here: 89.3 us
  blocking collectives  30.6 us (34%)
  starting transfers between devices  30.2 us (34%)
  Pallas kernels  20 us (22%)
  waiting for transfers between devices  8.39 us (9%)
    all_to_all x2, blocking collectives, spread_sums(): return lax.all_to_all(copies, axes, 0, 0, tiled=True)  30.6 us
    ppermute x12, starting transfers between devices, exchange(): return [lax.ppermute(s, ALL, p) for s, p in zip(sends, perms)]  30.2 us
    ppermute x12, waiting for transfers between devices, exchange(): return [lax.ppermute(s, ALL, p) for s, p in zip(sends, perms)]  8.39 us
    pallas_call x1, Pallas kernels, local(): pl.pallas_call(step2_kernel, out_shape=[table_shape, table_shape, sums_sh...  4.14 us
    pallas_call x1, Pallas kernels, local(): pl.pallas_call(step1_kernel, out_shape=[table_shape, table_shape, wide, s...  4.14 us
    pallas_call x1, Pallas kernels, local(): pl.pallas_call(step3_kernel, out_shape=[table_shape, wide, sums_shape(3)]...  4.12 us
    pallas_call x1, Pallas kernels, local(): pl.pallas_call(load_kernel, out_shape=[table_shape, pltpu.VMEM(tile_value...  3.73 us
    pallas_call x1, Pallas kernels, local(): pl.pallas_call(first_kernel, out_shape=send_shape, in_specs=[SMEM, HBM],...  2.14 us
  transfers between devices with their start and end apart: 12, of which 3 were waited for; matrix products, arithmetic and copies ran while one was open for 0% of the time, Pallas kernels for 4%

profile of v1, /device:TPU:32, one launch (start us, length us, event | category | flops | bytes accessed | tf_op | source)
XLA Modules:
  0.0 89.3 jit_solution(8751682847792132023)
XLA Ops:
  0.0 2.1 %first.1 = (bf16[4,128,256]{2,1,0:T(8,128)(2,1)S(1)}, bf16[4,128,256]{2,1,0:T(8,128)(2,1)S(1)}, bf16[4,128,256]{2,1,0:T(8,128)(2,1)S(1)}, bf16[4,128,256]{2,1,0:T(8,128)(2,1)S(1)}) custom-call(s32[1,4,4]{2,1,0:T(4,128)} %halo.5, bf16[16,128,256]{2,1,0:T(8,128)(2,1)} %bitcast.2), custom_call_target="tpu_custom_call" | custom-call | tf_op jit(solution)/shard_map/first/pallas_call | solution.py:224
  2.1 1.5 %collective-permute-start = (bf16[4,128,256]{2,1,0:T(8,128)(2,1)S(1)}, bf16[4,128,256]{2,1,0:T(8,128)(2,1)S(1)}, u32[]{:S(2)}, u32[]{:S(2)}) collective-permute-start(bf16[4,128,256]{2,1,0:T(8,128)(2,1)S(1)} %get-tuple-element.29), channel_id=1, source_target_pairs={{0,1},{1,0},{2,3},{3,2},{4,5},{5,4},{6,7},{7,6},{8,9},{9,8},{10,11... | collective-permute-start | bytes 786440 | tf_op jit(solution)/shard_map/ppermute | solution.py:183
  3.7 0.8 collective-permute-start.1
  4.5 1.4 %collective-permute-start.2 = (bf16[4,128,256]{2,1,0:T(8,128)(2,1)S(1)}, bf16[4,128,256]{2,1,0:T(8,128)(2,1)S(1)}, u32[]{:S(2)}, u32[]{:S(2)}) collective-permute-start(bf16[4,128,256]{2,1,0:T(8,128)(2,1)S(1)} %get-tuple-element.31), channel_id=1, source_target_pairs={{0,4},{1,5},{2,6},{3,7},{4,0},{5,1},{6,2},{7,3},{8,12},{9,13},{10,... | collective-permute-start | bytes 786440 | tf_op jit(solution)/shard_map/ppermute | solution.py:183
  5.9 7.0 %collective-permute-start.3 = (bf16[4,128,256]{2,1,0:T(8,128)(2,1)S(1)}, bf16[4,128,256]{2,1,0:T(8,128)(2,1)S(1)}, u32[]{:S(2)}, u32[]{:S(2)}) collective-permute-start(bf16[4,128,256]{2,1,0:T(8,128)(2,1)S(1)} %get-tuple-element.32), channel_id=1, source_target_pairs={{0,252},{1,253},{2,254},{3,255},{4,8},{5,9},{6,10},{7,11},{8,4},{9... | collective-permute-start | bytes 786440 | tf_op jit(solution)/shard_map/ppermute | solution.py:183
  12.9 3.7 %load.1 = (bf16[32,128,256]{2,1,0:T(8,128)(2,1)S(1)}, bf16[256,128,128]{2,1,0:T(8,128)(2,1)S(1)}) custom-call(bf16[16,128,256]{2,1,0:T(8,128)(2,1)} %bitcast.3, bf16[256,128,128]{2,1,0:T(8,128)(2,1)} %tiles.1), custom_call_target="tpu_custom_call" | custom-call | tf_op jit(solution)/shard_map/load/pallas_call | solution.py:234
  16.6 0.0 collective-permute-done.1.rb
  16.7 0.0 collective-permute-done.2.rc
  16.7 0.3 collective-permute-done.3.rd
  16.9 4.1 %step1.1 = (bf16[32,128,256]{2,1,0:T(8,128)(2,1)S(1)}, bf16[32,128,256]{2,1,0:T(8,128)(2,1)S(1)}, f32[16,128,256]{2,1,0:T(8,128)S(1)}, f32[3,256]{1,0:T(4,128)S(...) custom-call(s32[256]{0:T(256)} %cols.5, ...), custom_call_target="tpu_custom_call", output_to_operand_aliasing={{0}: (3, {})} | custom-call | tf_op jit(solution)/shard_map/step1/pallas_call | solution.py:243
  21.1 0.1 collective-permute-start.4
  21.2 0.1 collective-permute-start.5
  21.3 0.1 collective-permute-start.6
  21.4 9.0 %collective-permute-start.7 = (bf16[4,128,256]{2,1,0:T(8,128)(2,1)S(1)}, bf16[4,128,256]{2,1,0:T(8,128)(2,1)S(1)}, u32[]{:S(2)}, u32[]{:S(2)}) collective-permute-start(bf16[4,128,256]{2,1,0:T(8,128)(2,1)S(1)} %get-tuple-element.39), channel_id=1, source_target_pairs={{0,252},{1,253},{2,254},{3,255},{4,8},{5,9},{6,10},{7,11},{8,4},{9... | collective-permute-start | bytes 786440 | tf_op jit(solution)/shard_map/ppermute | solution.py:183
  30.4 4.0 %collective-permute-done.7.rd = bf16[4,128,256]{2,1,0:T(8,128)(2,1)S(1)} collective-permute-done((bf16[4,128,256]{2,1,0:T(8,128)(2,1)S(1)}, bf16[4,128,256]{2,1,0:T(8,128)(2,1)S(1)}, u32[]{:S(2)}, u32[]{:S(2)}) %collective-permute-start.7) | collective-permute-done | bytes 262176 | tf_op jit(solution)/shard_map/ppermute | solution.py:183
  34.5 4.1 %step2.1 = (bf16[32,128,256]{2,1,0:T(8,128)(2,1)S(1)}, bf16[32,128,256]{2,1,0:T(8,128)(2,1)S(1)}, f32[2,256]{1,0:T(2,128)S(1)}, bf16[4,128,256]{2,1,0:T(8,128)(2...) custom-call(s32[256]{0:T(256)} %cols.5, ...), custom_call_target="tpu_custom_call", output_to_operand_aliasing={{0}: (4, {})} | custom-call | tf_op jit(solution)/shard_map/step2/pallas_call | solution.py:253
  38.6 0.1 collective-permute-start.8
  38.7 1.7 %collective-permute-start.9 = (bf16[4,128,256]{2,1,0:T(8,128)(2,1)S(1)}, bf16[4,128,256]{2,1,0:T(8,128)(2,1)S(1)}, u32[]{:S(2)}, u32[]{:S(2)}) collective-permute-start(bf16[4,128,256]{2,1,0:T(8,128)(2,1)S(1)} %get-tuple-element.44), channel_id=1, source_target_pairs={{0,255},{1,2},{2,1},{3,4},{4,3},{5,6},{6,5},{7,8},{8,7},{9,10},{10... | collective-permute-start | bytes 786440 | tf_op jit(solution)/shard_map/ppermute | solution.py:183
  40.4 8.4 %collective-permute-start.11 = (bf16[4,128,256]{2,1,0:T(8,128)(2,1)S(1)}, bf16[4,128,256]{2,1,0:T(8,128)(2,1)S(1)}, u32[]{:S(2)}, u32[]{:S(2)}) collective-permute-start(bf16[4,128,256]{2,1,0:T(8,128)(2,1)S(1)} %get-tuple-element.46), channel_id=1, source_target_pairs={{0,252},{1,253},{2,254},{3,255},{4,8},{5,9},{6,10},{7,11},{8,4},{9... | collective-permute-start | bytes 786440 | tf_op jit(solution)/shard_map/ppermute | solution.py:183
  48.8 4.0 %collective-permute-done.11.rd = bf16[4,128,256]{2,1,0:T(8,128)(2,1)S(1)} collective-permute-done((bf16[4,128,256]{2,1,0:T(8,128)(2,1)S(1)}, bf16[4,128,256]{2,1,0:T(8,128)(2,1)S(1)}, u32[]{:S(2)}, u32[]{:S(2)}) %collective-permute-start.11) | collective-permute-done | bytes 262176 | tf_op jit(solution)/shard_map/ppermute | solution.py:183
  52.8 4.1 %step3.1 = (bf16[32,128,256]{2,1,0:T(8,128)(2,1)S(1)}, f32[16,128,256]{2,1,0:T(8,128)S(1)}, f32[3,256]{1,0:T(4,128)S(1)}) custom-call(s32[256]{0:T(256)} %cols.5, bf16[256,128,128]{2,1,0:T(8,128)(2,1)S(1)} %get-tuple-element.27.tiles, bf16[32,128,256]{2,1,0:T(8,128)(2,1)S(1)} %get-tuple-element.34.features, ...), custom_call_target="tpu_custom_call", output_to_operand_aliasing={{0}: (4, {})} | custom-call | tf_op jit(solution)/shard_map/step3/pallas_call | solution.py:263
  57.0 7.7 %all_to_all.10.sums = f32[8,8,256]{2,1,0:T(8,128)S(1)} all-to-all(f32[8,8,256]{2,1,0:T(8,128)S(1)} %copies.2), channel_id=1, replica_groups=mesh['y'=4,'z'=8,'c'=2,'x'=4] {'c','x'}, dimensions={0} | all-to-all | bytes 131072 | tf_op jit(solution)/shard_map/all_to_all | solution.py:205
  64.7 22.9 %all_to_all.11.sums = f32[32,8,256]{2,1,0:T(8,128)S(1)} all-to-all(f32[32,8,256]{2,1,0:T(8,128)S(1)} %copies.3), channel_id=1, replica_groups=mesh['y'=4,'z'=8,'c'=2,'x'=4] {'y','z'}, dimensions={0} | all-to-all | bytes 524288 | tf_op jit(solution)/shard_map/all_to_all | solution.py:205
  87.7 1.7 %last.1 = bf16[16,128,256]{2,1,0:T(8,128)(2,1)} custom-call(f32[32,8,256]{2,1,0:T(8,128)S(1)} %all_to_all.11.sums, bf16[32,128,256]{2,1,0:T(8,128)(2,1)S(1)} %get-tuple-element.34.features, f32[16,128,256]{2,1,0:T(8,128)S(1)} %get-tuple-element.41.held, f32[16,128,256]{2,1,0:T(8,128)S(1)} %get-tuple-element.48.spread), custom_call_target="tpu_custom_call" | custom-call | tf_op jit(solution)/shard_map/last/pallas_call | solution.py:274
  (10 shorter events, 0.1 us)
Async XLA Ops:
  2.1 14.5 %collective-permute-start = (bf16[4,128,256]{2,1,0:T(8,128)(2,1)S(1)}, bf16[4,128,256]{2,1,0:T(8,128)(2,1)S(1)}, u32[]{:S(2)}, u32[]{:S(2)}) collective-permute-start(bf16[4,128,256]{2,1,0:T(8,128)(2,1)S(1)} %get-tuple-element.29), channel_id=1, source_target_pairs={{0,1},{1,0},{2,3},{3,2},{4,5},{5,4},{6,7},{7,6},{8,9},{9,8},{10,11... | collective-permute-start | bytes 786440 | tf_op jit(solution)/shard_map/ppermute | solution.py:183
  3.7 13.0 %collective-permute-start.1 = (bf16[4,128,256]{2,1,0:T(8,128)(2,1)S(1)}, bf16[4,128,256]{2,1,0:T(8,128)(2,1)S(1)}, u32[]{:S(2)}, u32[]{:S(2)}) collective-permute-start(bf16[4,128,256]{2,1,0:T(8,128)(2,1)S(1)} %get-tuple-element.30), channel_id=1, source_target_pairs={{0,255},{1,2},{2,1},{3,4},{4,3},{5,6},{6,5},{7,8},{8,7},{9,10},{10... | collective-permute-start | bytes 786440 | tf_op jit(solution)/shard_map/ppermute | solution.py:183
  4.5 12.2 %collective-permute-start.2 = (bf16[4,128,256]{2,1,0:T(8,128)(2,1)S(1)}, bf16[4,128,256]{2,1,0:T(8,128)(2,1)S(1)}, u32[]{:S(2)}, u32[]{:S(2)}) collective-permute-start(bf16[4,128,256]{2,1,0:T(8,128)(2,1)S(1)} %get-tuple-element.31), channel_id=1, source_target_pairs={{0,4},{1,5},{2,6},{3,7},{4,0},{5,1},{6,2},{7,3},{8,12},{9,13},{10,... | collective-permute-start | bytes 786440 | tf_op jit(solution)/shard_map/ppermute | solution.py:183
  5.9 11.1 %collective-permute-start.3 = (bf16[4,128,256]{2,1,0:T(8,128)(2,1)S(1)}, bf16[4,128,256]{2,1,0:T(8,128)(2,1)S(1)}, u32[]{:S(2)}, u32[]{:S(2)}) collective-permute-start(bf16[4,128,256]{2,1,0:T(8,128)(2,1)S(1)} %get-tuple-element.32), channel_id=1, source_target_pairs={{0,252},{1,253},{2,254},{3,255},{4,8},{5,9},{6,10},{7,11},{8,4},{9... | collective-permute-start | bytes 786440 | tf_op jit(solution)/shard_map/ppermute | solution.py:183
  21.1 9.3 %collective-permute-start.4 = (bf16[4,128,256]{2,1,0:T(8,128)(2,1)S(1)}, bf16[4,128,256]{2,1,0:T(8,128)(2,1)S(1)}, u32[]{:S(2)}, u32[]{:S(2)}) collective-permute-start(bf16[4,128,256]{2,1,0:T(8,128)(2,1)S(1)} %get-tuple-element.36), channel_id=1, source_target_pairs={{0,1},{1,0},{2,3},{3,2},{4,5},{5,4},{6,7},{7,6},{8,9},{9,8},{10,11... | collective-permute-start | bytes 786440 | tf_op jit(solution)/shard_map/ppermute | solution.py:183
  21.2 9.2 %collective-permute-start.5 = (bf16[4,128,256]{2,1,0:T(8,128)(2,1)S(1)}, bf16[4,128,256]{2,1,0:T(8,128)(2,1)S(1)}, u32[]{:S(2)}, u32[]{:S(2)}) collective-permute-start(bf16[4,128,256]{2,1,0:T(8,128)(2,1)S(1)} %get-tuple-element.37), channel_id=1, source_target_pairs={{0,255},{1,2},{2,1},{3,4},{4,3},{5,6},{6,5},{7,8},{8,7},{9,10},{10... | collective-permute-start | bytes 786440 | tf_op jit(solution)/shard_map/ppermute | solution.py:183
  21.3 9.1 %collective-permute-start.6 = (bf16[4,128,256]{2,1,0:T(8,128)(2,1)S(1)}, bf16[4,128,256]{2,1,0:T(8,128)(2,1)S(1)}, u32[]{:S(2)}, u32[]{:S(2)}) collective-permute-start(bf16[4,128,256]{2,1,0:T(8,128)(2,1)S(1)} %get-tuple-element.38), channel_id=1, source_target_pairs={{0,4},{1,5},{2,6},{3,7},{4,0},{5,1},{6,2},{7,3},{8,12},{9,13},{10,... | collective-permute-start | bytes 786440 | tf_op jit(solution)/shard_map/ppermute | solution.py:183
  21.4 13.1 %collective-permute-start.7 = (bf16[4,128,256]{2,1,0:T(8,128)(2,1)S(1)}, bf16[4,128,256]{2,1,0:T(8,128)(2,1)S(1)}, u32[]{:S(2)}, u32[]{:S(2)}) collective-permute-start(bf16[4,128,256]{2,1,0:T(8,128)(2,1)S(1)} %get-tuple-element.39), channel_id=1, source_target_pairs={{0,252},{1,253},{2,254},{3,255},{4,8},{5,9},{6,10},{7,11},{8,4},{9... | collective-permute-start | bytes 786440 | tf_op jit(solution)/shard_map/ppermute | solution.py:183
  38.6 10.2 %collective-permute-start.8 = (bf16[4,128,256]{2,1,0:T(8,128)(2,1)S(1)}, bf16[4,128,256]{2,1,0:T(8,128)(2,1)S(1)}, u32[]{:S(2)}, u32[]{:S(2)}) collective-permute-start(bf16[4,128,256]{2,1,0:T(8,128)(2,1)S(1)} %get-tuple-element.43), channel_id=1, source_target_pairs={{0,1},{1,0},{2,3},{3,2},{4,5},{5,4},{6,7},{7,6},{8,9},{9,8},{10,11... | collective-permute-start | bytes 786440 | tf_op jit(solution)/shard_map/ppermute | solution.py:183
  38.7 10.1 %collective-permute-start.9 = (bf16[4,128,256]{2,1,0:T(8,128)(2,1)S(1)}, bf16[4,128,256]{2,1,0:T(8,128)(2,1)S(1)}, u32[]{:S(2)}, u32[]{:S(2)}) collective-permute-start(bf16[4,128,256]{2,1,0:T(8,128)(2,1)S(1)} %get-tuple-element.44), channel_id=1, source_target_pairs={{0,255},{1,2},{2,1},{3,4},{4,3},{5,6},{6,5},{7,8},{8,7},{9,10},{10... | collective-permute-start | bytes 786440 | tf_op jit(solution)/shard_map/ppermute | solution.py:183
  40.4 8.4 %collective-permute-start.10 = (bf16[4,128,256]{2,1,0:T(8,128)(2,1)S(1)}, bf16[4,128,256]{2,1,0:T(8,128)(2,1)S(1)}, u32[]{:S(2)}, u32[]{:S(2)}) collective-permute-start(bf16[4,128,256]{2,1,0:T(8,128)(2,1)S(1)} %get-tuple-element.45), channel_id=1, source_target_pairs={{0,4},{1,5},{2,6},{3,7},{4,0},{5,1},{6,2},{7,3},{8,12},{9,13},{10,... | collective-permute-start | bytes 786440 | tf_op jit(solution)/shard_map/ppermute | solution.py:183
  40.4 12.4 %collective-permute-start.11 = (bf16[4,128,256]{2,1,0:T(8,128)(2,1)S(1)}, bf16[4,128,256]{2,1,0:T(8,128)(2,1)S(1)}, u32[]{:S(2)}, u32[]{:S(2)}) collective-permute-start(bf16[4,128,256]{2,1,0:T(8,128)(2,1)S(1)} %get-tuple-element.46), channel_id=1, source_target_pairs={{0,252},{1,253},{2,254},{3,255},{4,8},{5,9},{6,10},{7,11},{8,4},{9... | collective-permute-start | bytes 786440 | tf_op jit(solution)/shard_map/ppermute | solution.py:183

commit v2 on v1

--- a/solution.py
+++ b/solution.py
@@ -11,7 +11,7 @@
 ALL = ("y", "z", "c", "x")
 LIMIT = 4 * 1024 * 1024
 TILE = 128
-ROWS_PER_STEP = 4
+ROWS_PER_STEP = 8
 
 VMEM = pl.BlockSpec(memory_space=pltpu.VMEM)
 SMEM = pl.BlockSpec(memory_space=pltpu.SMEM)
@@ -42,23 +42,24 @@
             send[j] = table[halo[0, to, j]]
 
 
-def first_kernel(halo, features, *sends_and_sems):
-    *sends, sems = sends_and_sems
-    copies = []
-    for k, (to, _) in enumerate(send_lists()):
-        for j in range(sends[k].shape[0]):
-            copies.append(
-                pltpu.make_async_copy(features.at[halo[0, to, j]], sends[k].at[j], sems.at[k, j])
-            )
-            copies[-1].start()
+def first_kernel(halo, features, table, *sends_and_scratch):
+    *sends, lists, sems = sends_and_scratch
+    copies = [
+        pltpu.make_async_copy(halo, lists, sems.at[0]),
+        pltpu.make_async_copy(features, table.at[pl.ds(0, features.shape[0])], sems.at[1]),
+    ]
+    for copy in copies:
+        copy.start()
     for copy in copies:
         copy.wait()
-
-
-def load_kernel(features, tiles, table, kept, sems):
+    pack(lists, table, sends)
+
+
+def load_kernel(tiles, cols, halo, kept, cols_out, halo_out, sems):
     copies = [
-        pltpu.make_async_copy(features, table.at[pl.ds(0, features.shape[0])], sems.at[0]),
-        pltpu.make_async_copy(tiles, kept, sems.at[1]),
+        pltpu.make_async_copy(cols, cols_out, sems.at[0]),
+        pltpu.make_async_copy(halo, halo_out, sems.at[1]),
+        pltpu.make_async_copy(tiles, kept, sems.at[2]),
     ]
     for copy in copies:
         copy.start()
@@ -97,9 +98,9 @@
     return lax.fori_loop(0, nblocks // ROWS_PER_STEP, step, zero)
 
 
-def write_sums(out, sums):
+def write_sums(out, sums, at=0):
     for k, s in enumerate(sums):
-        out[pl.ds(k, 1), :] = jnp.sum(s, axis=0, keepdims=True)
+        out[pl.ds(at + k, 1), :] = jnp.sum(s, axis=0, keepdims=True)
 
 
 def step1_kernel(cols, halo, tiles, _, ra, rb, rc, rd, table, table_out, held, sums_out, *sends):
@@ -135,7 +136,7 @@
     pack(halo, table_out, sends)
 
 
-def step3_kernel(cols, tiles, features, held, _, ra, rb, rc, rd, table, spread_out, sums_out):
+def step3_kernel(cols, tiles, features, held, _, ra, rb, rc, rd, sums1, sums2, table, spread_out, sums_out):
     nblocks = held.shape[0]
     per_row = tiles.shape[0] // nblocks
     gather_halo(table, (ra, rb, rc, rd), nblocks)
@@ -147,10 +148,13 @@
         new = (spread * spread, spread * start, spread * held[row])
         return tuple(s + fold(n) for s, n in zip(sums, new))
 
-    write_sums(sums_out, over_rows(nblocks, 3, body))
-
-
-def last_kernel(vertices, sums, features, held, spread, out):
+    first, second = sums1.shape[0], sums2.shape[0]
+    sums_out[pl.ds(0, first)] = sums1[...]
+    sums_out[pl.ds(first, second)] = sums2[...]
+    write_sums(sums_out, over_rows(nblocks, 3, body), first + second)
+
+
+def last_kernel(vertices, sums, features, held, spread, out, staged, sems):
     total = jnp.sum(sums[...], axis=0)
     ff, yf, yy, ww, wf, vv, vf, vy = [total[k : k + 1] for k in range(8)]
 
@@ -166,12 +170,17 @@
     b = 0.09 * s2 * s3
     c = 0.1 * s3
 
-    def body(row, carry):
-        start = features[row].astype(jnp.float32)
-        out[row] = (a * spread[row] + b * held[row] + c * start).astype(jnp.bfloat16)
-        return carry
-
-    lax.fori_loop(0, out.shape[0], body, 0)
+    copies = []
+    size = out.shape[0] // sems.shape[0]
+    for k in range(sems.shape[0]):
+        for row in range(k * size, (k + 1) * size):
+            start = features[row].astype(jnp.float32)
+            staged[row] = (a * spread[row] + b * held[row] + c * start).astype(jnp.bfloat16)
+        part = pl.ds(k * size, size)
+        copies.append(pltpu.make_async_copy(staged.at[part], out.at[part], sems.at[k]))
+        copies[-1].start()
+    for copy in copies:
+        copy.wait()
 
 
 def in_hbm(array):
@@ -183,9 +192,8 @@
     return [lax.ppermute(s, ALL, p) for s, p in zip(sends, perms)]
 
 
-def join_kernel(first, second, third, out):
-    joined = jnp.concatenate([first[...], second[...], third[...]], axis=0)
-    out[...] = jnp.broadcast_to(joined[None], out.shape)
+def pair_kernel(own, partner, out):
+    out[...] = jnp.broadcast_to((own[...] + partner[...])[None], out.shape)
 
 
 def add_kernel(sums, out):
@@ -221,25 +229,32 @@
     def sums_shape(count):
         return pltpu.VMEM((count, classes), jnp.float32)
 
-    sends = pl.pallas_call(
+    table0, *sends = pl.pallas_call(
         first_kernel,
-        out_shape=send_shape,
-        in_specs=[SMEM, HBM],
-        out_specs=[VMEM] * 4,
-        scratch_shapes=[pltpu.SemaphoreType.DMA((peers, slots))],
+        out_shape=[table_shape] + send_shape,
+        in_specs=[HBM, HBM],
+        out_specs=[VMEM] * 5,
+        scratch_shapes=[
+            pltpu.SMEM(halo_rows.shape, jnp.int32),
+            pltpu.SemaphoreType.DMA((2,)),
+        ],
         compiler_params=PARAMS,
         name="first",
     )(halo_rows, blocks)
     received = exchange(sends)
-    table0, kept = pl.pallas_call(
+    kept, tile_cols, halo_rows = pl.pallas_call(
         load_kernel,
-        out_shape=[table_shape, pltpu.VMEM(tile_values.shape, tile_values.dtype)],
-        in_specs=[HBM, HBM],
-        out_specs=[VMEM, VMEM],
-        scratch_shapes=[pltpu.SemaphoreType.DMA((2,))],
+        out_shape=[
+            pltpu.VMEM(tile_values.shape, tile_values.dtype),
+            pltpu.SMEM(tile_cols.shape, jnp.int32),
+            pltpu.SMEM(halo_rows.shape, jnp.int32),
+        ],
+        in_specs=[HBM] * 3,
+        out_specs=[VMEM, SMEM, SMEM],
+        scratch_shapes=[pltpu.SemaphoreType.DMA((3,))],
         compiler_params=PARAMS,
         name="load",
-    )(blocks, in_hbm(tile_values))
+    )(in_hbm(tile_values), tile_cols, halo_rows)
     table0, table1, held, sums1, *sends = pl.pallas_call(
         step1_kernel,
         out_shape=[table_shape, table_shape, wide, sums_shape(3)] + send_shape,
@@ -260,22 +275,27 @@
         name="step2",
     )(tile_cols, halo_rows, kept, table0, table1, *received)
     received = exchange(sends)
-    _, spread, sums3 = pl.pallas_call(
+    _, spread, sums = pl.pallas_call(
         step3_kernel,
-        out_shape=[table_shape, wide, sums_shape(3)],
+        out_shape=[table_shape, wide, sums_shape(8)],
         input_output_aliases={4: 0},
-        in_specs=[SMEM] + [VMEM] * 8,
+        in_specs=[SMEM] + [VMEM] * 10,
         out_specs=[VMEM] * 3,
         compiler_params=PARAMS,
         name="step3",
-    )(tile_cols, kept, table0, held, table2, *received)
-    sums = spread_sums(join_kernel, ("c", "x"), sums1, sums2, sums3)
-    sums = spread_sums(add_kernel, ("y", "z"), sums)
+    )(tile_cols, kept, table0, held, table2, *received, sums1, sums2)
+    partner = lax.ppermute(sums, "c", [(0, 1), (1, 0)])
+    sums = spread_sums(pair_kernel, ("y", "x"), sums, partner)
+    sums = spread_sums(add_kernel, ("z",), sums)
     out = pl.pallas_call(
         functools.partial(last_kernel, vertices),
         out_shape=jax.ShapeDtypeStruct((nblocks, tile, classes), jnp.bfloat16),
         in_specs=[VMEM] * 4,
-        out_specs=VMEM,
+        out_specs=HBM,
+        scratch_shapes=[
+            pltpu.VMEM((nblocks, tile, classes), jnp.bfloat16),
+            pltpu.SemaphoreType.DMA((4,)),
+        ],
         compiler_params=PARAMS,
         name="last",
     )(sums, table0, held, spread)

time: 89.6 us -> 83.5 us (0.932)
  Pallas kernels: 20 us -> 14.9 us
  blocking collectives: 30.6 us -> 27.6 us
  waiting for transfers between devices: 8.39 us -> 9.87 us
    all_to_all x2, blocking collectives: 30.6 us -> 27.6 us  [spread_sums(): return lax.all_to_all(copies, axes, 0, 0, tiled=True)]
    pallas_call x3, Pallas kernels: 9.99 us -> 7.61 us  [the longest x1 3.41 us: local(): pl.pallas_call(load_kernel, out_shape=[pltpu.VMEM(tile_values.shape, tile...]
    pallas_call x1, Pallas kernels: 4.14 us -> 2.86 us  [local(): pl.pallas_call(step2_kernel, out_shape=[table_shape, table_shape, sums_sh...]
    ppermute x0 -> x1, waiting for transfers between devices: none -> 1.16 us  [local(): partner = lax.ppermute(sums, 'c', [(0, 1), (1, 0)])]
    pallas_call x1, Pallas kernels: 4.14 us -> 3.1 us  [local(): pl.pallas_call(step1_kernel, out_shape=[table_shape, table_shape, wide, s...]
  transfers between devices with their start and end apart: 12 -> 13, of which waited for: 3 -> 4; matrix products, arithmetic and copies ran while one was open for 0% -> 0% of each run, Pallas kernels for 4% -> 4%
where the time goes in v2:
time: 83.5 us; the launch traced here: 82.9 us
  starting transfers between devices  30.3 us (36%)
  blocking collectives  27.6 us (33%)
  Pallas kernels  14.9 us (18%)
  waiting for transfers between devices  9.87 us (12%)
    ppermute x12, starting transfers between devices, exchange(): return [lax.ppermute(s, ALL, p) for s, p in zip(sends, perms)]  30.2 us
    all_to_all x2, blocking collectives, spread_sums(): return lax.all_to_all(copies, axes, 0, 0, tiled=True)  27.6 us
    ppermute x12, waiting for transfers between devices, exchange(): return [lax.ppermute(s, ALL, p) for s, p in zip(sends, perms)]  8.71 us
    pallas_call x1, Pallas kernels, local(): pl.pallas_call(load_kernel, out_shape=[pltpu.VMEM(tile_values.shape, tile...  3.41 us
    pallas_call x1, Pallas kernels, local(): pl.pallas_call(step1_kernel, out_shape=[table_shape, table_shape, wide, s...  3.1 us
    pallas_call x1, Pallas kernels, local(): pl.pallas_call(step3_kernel, out_shape=[table_shape, wide, sums_shape(8)]...  2.89 us
    pallas_call x1, Pallas kernels, local(): pl.pallas_call(step2_kernel, out_shape=[table_shape, table_shape, sums_sh...  2.86 us
  transfers between devices with their start and end apart: 13, of which 4 were waited for; matrix products, arithmetic and copies ran while one was open for 0% of the time, Pallas kernels for 4%

profile of v2, /device:TPU:32, one launch (start us, length us, event | category | flops | bytes accessed | tf_op | source)
XLA Modules:
  0.0 82.9 jit_solution(11065914967644829615)
XLA Ops:
  0.0 1.3 %first.1 = (bf16[32,128,256]{2,1,0:T(8,128)(2,1)S(1)}, bf16[4,128,256]{2,1,0:T(8,128)(2,1)S(1)}, bf16[4,128,256]{2,1,0:T(8,128)(2,1)S(1)}, bf16[4,128,256]{2,1,0:T(8,128)(2,1)S(1)}, bf16[4,128,256]{2,1,0:T(8,128)(2,1)S(1)}) custom-call(s32[1,4,4]{2,1,0:T(4,128)} %halo.3, bf16[16,128,256]{2,1,0:T(8,128)(2,1)} %bitcast.2), custom_call_target="tpu_custom_call" | custom-call | tf_op jit(solution)/shard_map/first/pallas_call | solution.py:232
  1.3 1.6 %collective-permute-start = (bf16[4,128,256]{2,1,0:T(8,128)(2,1)S(1)}, bf16[4,128,256]{2,1,0:T(8,128)(2,1)S(1)}, u32[]{:S(2)}, u32[]{:S(2)}) collective-permute-start(bf16[4,128,256]{2,1,0:T(8,128)(2,1)S(1)} %get-tuple-element.33), channel_id=1, source_target_pairs={{0,1},{1,0},{2,3},{3,2},{4,5},{5,4},{6,7},{7,6},{8,9},{9,8},{10,11... | collective-permute-start | bytes 786440 | tf_op jit(solution)/shard_map/ppermute | solution.py:192
  2.9 0.8 collective-permute-start.1
  3.7 1.4 %collective-permute-start.2 = (bf16[4,128,256]{2,1,0:T(8,128)(2,1)S(1)}, bf16[4,128,256]{2,1,0:T(8,128)(2,1)S(1)}, u32[]{:S(2)}, u32[]{:S(2)}) collective-permute-start(bf16[4,128,256]{2,1,0:T(8,128)(2,1)S(1)} %get-tuple-element.35), channel_id=1, source_target_pairs={{0,4},{1,5},{2,6},{3,7},{4,0},{5,1},{6,2},{7,3},{8,12},{9,13},{10,... | collective-permute-start | bytes 786440 | tf_op jit(solution)/shard_map/ppermute | solution.py:192
  5.1 7.0 %collective-permute-start.3 = (bf16[4,128,256]{2,1,0:T(8,128)(2,1)S(1)}, bf16[4,128,256]{2,1,0:T(8,128)(2,1)S(1)}, u32[]{:S(2)}, u32[]{:S(2)}) collective-permute-start(bf16[4,128,256]{2,1,0:T(8,128)(2,1)S(1)} %get-tuple-element.36), channel_id=1, source_target_pairs={{0,252},{1,253},{2,254},{3,255},{4,8},{5,9},{6,10},{7,11},{8,4},{9... | collective-permute-start | bytes 786440 | tf_op jit(solution)/shard_map/ppermute | solution.py:192
  12.1 3.4 %load.1 = (bf16[256,128,128]{2,1,0:T(8,128)(2,1)S(1)}, s32[256]{0:T(256)S(4)}, s32[1,4,4]{2,1,0:T(4,128)S(4)}) custom-call(bf16[256,128,128]{2,1,0:T(8,128)(2,1)} %tiles.1, s32[256]{0:T(256)} %cols.1, s32[1,4,4]{2,1,0:T(4,128)} %halo.3), custom_call_target="tpu_custom_call" | custom-call | tf_op jit(solution)/shard_map/load/pallas_call | solution.py:245
  15.6 0.6 collective-permute-done.3.rd
  16.2 3.1 %step1.1 = (bf16[32,128,256]{2,1,0:T(8,128)(2,1)S(1)}, bf16[32,128,256]{2,1,0:T(8,128)(2,1)S(1)}, f32[16,128,256]{2,1,0:T(8,128)S(1)}, f32[3,256]{1,0:T(4,128)S(...) custom-call(s32[256]{0:T(256)S(4)} %get-tuple-element.29.cols, ...), custom_call_target="tpu_custom_call", output_to_operand_aliasing={{0}: (3, {})} | custom-call | tf_op jit(solution)/shard_map/step1/pallas_call | solution.py:258
  19.3 0.1 collective-permute-start.4
  19.4 0.1 collective-permute-start.5
  19.5 0.1 collective-permute-start.6
  19.6 9.0 %collective-permute-start.7 = (bf16[4,128,256]{2,1,0:T(8,128)(2,1)S(1)}, bf16[4,128,256]{2,1,0:T(8,128)(2,1)S(1)}, u32[]{:S(2)}, u32[]{:S(2)}) collective-permute-start(bf16[4,128,256]{2,1,0:T(8,128)(2,1)S(1)} %get-tuple-element.43), channel_id=1, source_target_pairs={{0,252},{1,253},{2,254},{3,255},{4,8},{5,9},{6,10},{7,11},{8,4},{9... | collective-permute-start | bytes 786440 | tf_op jit(solution)/shard_map/ppermute | solution.py:192
  28.6 4.0 %collective-permute-done.7.rd = bf16[4,128,256]{2,1,0:T(8,128)(2,1)S(1)} collective-permute-done((bf16[4,128,256]{2,1,0:T(8,128)(2,1)S(1)}, bf16[4,128,256]{2,1,0:T(8,128)(2,1)S(1)}, u32[]{:S(2)}, u32[]{:S(2)}) %collective-permute-start.7) | collective-permute-done | bytes 262176 | tf_op jit(solution)/shard_map/ppermute | solution.py:192
  32.7 2.9 %step2.1 = (bf16[32,128,256]{2,1,0:T(8,128)(2,1)S(1)}, bf16[32,128,256]{2,1,0:T(8,128)(2,1)S(1)}, f32[2,256]{1,0:T(2,128)S(1)}, bf16[4,128,256]{2,1,0:T(8,128)(2...) custom-call(s32[256]{0:T(256)S(4)} %get-tuple-element.29.cols, ...), custom_call_target="tpu_custom_call", output_to_operand_aliasing={{0}: (4, {})} | custom-call | tf_op jit(solution)/shard_map/step2/pallas_call | solution.py:268
  35.5 0.1 collective-permute-start.8
  35.6 1.7 %collective-permute-start.9 = (bf16[4,128,256]{2,1,0:T(8,128)(2,1)S(1)}, bf16[4,128,256]{2,1,0:T(8,128)(2,1)S(1)}, u32[]{:S(2)}, u32[]{:S(2)}) collective-permute-start(bf16[4,128,256]{2,1,0:T(8,128)(2,1)S(1)} %get-tuple-element.46), channel_id=1, source_target_pairs={{0,255},{1,2},{2,1},{3,4},{4,3},{5,6},{6,5},{7,8},{8,7},{9,10},{10... | collective-permute-start | bytes 786440 | tf_op jit(solution)/shard_map/ppermute | solution.py:192
  37.3 8.4 %collective-permute-start.11 = (bf16[4,128,256]{2,1,0:T(8,128)(2,1)S(1)}, bf16[4,128,256]{2,1,0:T(8,128)(2,1)S(1)}, u32[]{:S(2)}, u32[]{:S(2)}) collective-permute-start(bf16[4,128,256]{2,1,0:T(8,128)(2,1)S(1)} %get-tuple-element.48), channel_id=1, source_target_pairs={{0,252},{1,253},{2,254},{3,255},{4,8},{5,9},{6,10},{7,11},{8,4},{9... | collective-permute-start | bytes 786440 | tf_op jit(solution)/shard_map/ppermute | solution.py:192
  45.7 4.0 %collective-permute-done.11.rd = bf16[4,128,256]{2,1,0:T(8,128)(2,1)S(1)} collective-permute-done((bf16[4,128,256]{2,1,0:T(8,128)(2,1)S(1)}, bf16[4,128,256]{2,1,0:T(8,128)(2,1)S(1)}, u32[]{:S(2)}, u32[]{:S(2)}) %collective-permute-start.11) | collective-permute-done | bytes 262176 | tf_op jit(solution)/shard_map/ppermute | solution.py:192
  49.7 2.9 %step3.1 = (bf16[32,128,256]{2,1,0:T(8,128)(2,1)S(1)}, f32[16,128,256]{2,1,0:T(8,128)S(1)}, f32[8,256]{1,0:T(8,128)S(1)}) custom-call(s32[256]{0:T(256)S(4)} %get-tuple-element.29.cols, bf16[256,128,128]{2,1,0:T(8,128)(2,1)S(1)} %get-tuple-element.30.tiles, bf16[32,128,256]{2,1,0:T(8,128)(2,1)S(1)} %get-tuple-element.37.features, ...), custom_call_target="tpu_custom_call", output_to_operand_aliasing={{0}: (4, {})} | custom-call | tf_op jit(solution)/shard_map/step3/pallas_call | solution.py:278
  52.6 0.1 collective-permute-start.12
  52.7 1.2 %collective-permute-done.12.partner = f32[8,256]{1,0:T(8,128)S(1)} collective-permute-done((f32[8,256]{1,0:T(8,128)S(1)}, f32[8,256]{1,0:T(8,128)S(1)}, u32[]{:S(2)}, u32[]{:S(2)}) %collective-permute-start.12) | collective-permute-done | bytes 8224 | tf_op jit(solution)/shard_map/ppermute | solution.py:287
  53.9 10.6 %all_to_all.10.sums = f32[16,8,256]{2,1,0:T(8,128)S(1)} all-to-all(f32[16,8,256]{2,1,0:T(8,128)S(1)} %copies.2), channel_id=1, replica_groups=mesh['y'=4,'z'=8,'c'=2,'x'=4] {'y','x'}, dimensions={0} | all-to-all | bytes 262144 | tf_op jit(solution)/shard_map/all_to_all | solution.py:213
  64.5 17.1 %all_to_all.11.sums = f32[8,8,256]{2,1,0:T(8,128)S(1)} all-to-all(f32[8,8,256]{2,1,0:T(8,128)S(1)} %copies.3), channel_id=1, replica_groups=mesh['y'=4,'z'=8,'c'=2,'x'=4] {'z'}, dimensions={0} | all-to-all | bytes 131072 | tf_op jit(solution)/shard_map/all_to_all | solution.py:213
  81.6 1.3 %last.1 = bf16[16,128,256]{2,1,0:T(8,128)(2,1)} custom-call(f32[8,8,256]{2,1,0:T(8,128)S(1)} %all_to_all.11.sums, bf16[32,128,256]{2,1,0:T(8,128)(2,1)S(1)} %get-tuple-element.37.features, f32[16,128,256]{2,1,0:T(8,128)S(1)} %get-tuple-element.38.held, f32[16,128,256]{2,1,0:T(8,128)S(1)} %get-tuple-element.52.spread), custom_call_target="tpu_custom_call" | custom-call | tf_op jit(solution)/shard_map/last/pallas_call | solution.py:290
  (12 shorter events, 0.1 us)
Async XLA Ops:
  1.3 14.2 %collective-permute-start = (bf16[4,128,256]{2,1,0:T(8,128)(2,1)S(1)}, bf16[4,128,256]{2,1,0:T(8,128)(2,1)S(1)}, u32[]{:S(2)}, u32[]{:S(2)}) collective-permute-start(bf16[4,128,256]{2,1,0:T(8,128)(2,1)S(1)} %get-tuple-element.33), channel_id=1, source_target_pairs={{0,1},{1,0},{2,3},{3,2},{4,5},{5,4},{6,7},{7,6},{8,9},{9,8},{10,11... | collective-permute-start | bytes 786440 | tf_op jit(solution)/shard_map/ppermute | solution.py:192
  2.9 12.7 %collective-permute-start.1 = (bf16[4,128,256]{2,1,0:T(8,128)(2,1)S(1)}, bf16[4,128,256]{2,1,0:T(8,128)(2,1)S(1)}, u32[]{:S(2)}, u32[]{:S(2)}) collective-permute-start(bf16[4,128,256]{2,1,0:T(8,128)(2,1)S(1)} %get-tuple-element.34), channel_id=1, source_target_pairs={{0,255},{1,2},{2,1},{3,4},{4,3},{5,6},{6,5},{7,8},{8,7},{9,10},{10... | collective-permute-start | bytes 786440 | tf_op jit(solution)/shard_map/ppermute | solution.py:192
  3.7 11.9 %collective-permute-start.2 = (bf16[4,128,256]{2,1,0:T(8,128)(2,1)S(1)}, bf16[4,128,256]{2,1,0:T(8,128)(2,1)S(1)}, u32[]{:S(2)}, u32[]{:S(2)}) collective-permute-start(bf16[4,128,256]{2,1,0:T(8,128)(2,1)S(1)} %get-tuple-element.35), channel_id=1, source_target_pairs={{0,4},{1,5},{2,6},{3,7},{4,0},{5,1},{6,2},{7,3},{8,12},{9,13},{10,... | collective-permute-start | bytes 786440 | tf_op jit(solution)/shard_map/ppermute | solution.py:192
  5.1 11.1 %collective-permute-start.3 = (bf16[4,128,256]{2,1,0:T(8,128)(2,1)S(1)}, bf16[4,128,256]{2,1,0:T(8,128)(2,1)S(1)}, u32[]{:S(2)}, u32[]{:S(2)}) collective-permute-start(bf16[4,128,256]{2,1,0:T(8,128)(2,1)S(1)} %get-tuple-element.36), channel_id=1, source_target_pairs={{0,252},{1,253},{2,254},{3,255},{4,8},{5,9},{6,10},{7,11},{8,4},{9... | collective-permute-start | bytes 786440 | tf_op jit(solution)/shard_map/ppermute | solution.py:192
  19.3 9.3 %collective-permute-start.4 = (bf16[4,128,256]{2,1,0:T(8,128)(2,1)S(1)}, bf16[4,128,256]{2,1,0:T(8,128)(2,1)S(1)}, u32[]{:S(2)}, u32[]{:S(2)}) collective-permute-start(bf16[4,128,256]{2,1,0:T(8,128)(2,1)S(1)} %get-tuple-element.40), channel_id=1, source_target_pairs={{0,1},{1,0},{2,3},{3,2},{4,5},{5,4},{6,7},{7,6},{8,9},{9,8},{10,11... | collective-permute-start | bytes 786440 | tf_op jit(solution)/shard_map/ppermute | solution.py:192
  19.4 9.2 %collective-permute-start.5 = (bf16[4,128,256]{2,1,0:T(8,128)(2,1)S(1)}, bf16[4,128,256]{2,1,0:T(8,128)(2,1)S(1)}, u32[]{:S(2)}, u32[]{:S(2)}) collective-permute-start(bf16[4,128,256]{2,1,0:T(8,128)(2,1)S(1)} %get-tuple-element.41), channel_id=1, source_target_pairs={{0,255},{1,2},{2,1},{3,4},{4,3},{5,6},{6,5},{7,8},{8,7},{9,10},{10... | collective-permute-start | bytes 786440 | tf_op jit(solution)/shard_map/ppermute | solution.py:192
  19.5 9.1 %collective-permute-start.6 = (bf16[4,128,256]{2,1,0:T(8,128)(2,1)S(1)}, bf16[4,128,256]{2,1,0:T(8,128)(2,1)S(1)}, u32[]{:S(2)}, u32[]{:S(2)}) collective-permute-start(bf16[4,128,256]{2,1,0:T(8,128)(2,1)S(1)} %get-tuple-element.42), channel_id=1, source_target_pairs={{0,4},{1,5},{2,6},{3,7},{4,0},{5,1},{6,2},{7,3},{8,12},{9,13},{10,... | collective-permute-start | bytes 786440 | tf_op jit(solution)/shard_map/ppermute | solution.py:192
  19.6 13.1 %collective-permute-start.7 = (bf16[4,128,256]{2,1,0:T(8,128)(2,1)S(1)}, bf16[4,128,256]{2,1,0:T(8,128)(2,1)S(1)}, u32[]{:S(2)}, u32[]{:S(2)}) collective-permute-start(bf16[4,128,256]{2,1,0:T(8,128)(2,1)S(1)} %get-tuple-element.43), channel_id=1, source_target_pairs={{0,252},{1,253},{2,254},{3,255},{4,8},{5,9},{6,10},{7,11},{8,4},{9... | collective-permute-start | bytes 786440 | tf_op jit(solution)/shard_map/ppermute | solution.py:192
  35.5 10.2 %collective-permute-start.8 = (bf16[4,128,256]{2,1,0:T(8,128)(2,1)S(1)}, bf16[4,128,256]{2,1,0:T(8,128)(2,1)S(1)}, u32[]{:S(2)}, u32[]{:S(2)}) collective-permute-start(bf16[4,128,256]{2,1,0:T(8,128)(2,1)S(1)} %get-tuple-element.45), channel_id=1, source_target_pairs={{0,1},{1,0},{2,3},{3,2},{4,5},{5,4},{6,7},{7,6},{8,9},{9,8},{10,11... | collective-permute-start | bytes 786440 | tf_op jit(solution)/shard_map/ppermute | solution.py:192
  35.6 10.1 %collective-permute-start.9 = (bf16[4,128,256]{2,1,0:T(8,128)(2,1)S(1)}, bf16[4,128,256]{2,1,0:T(8,128)(2,1)S(1)}, u32[]{:S(2)}, u32[]{:S(2)}) collective-permute-start(bf16[4,128,256]{2,1,0:T(8,128)(2,1)S(1)} %get-tuple-element.46), channel_id=1, source_target_pairs={{0,255},{1,2},{2,1},{3,4},{4,3},{5,6},{6,5},{7,8},{8,7},{9,10},{10... | collective-permute-start | bytes 786440 | tf_op jit(solution)/shard_map/ppermute | solution.py:192
  37.3 8.4 %collective-permute-start.10 = (bf16[4,128,256]{2,1,0:T(8,128)(2,1)S(1)}, bf16[4,128,256]{2,1,0:T(8,128)(2,1)S(1)}, u32[]{:S(2)}, u32[]{:S(2)}) collective-permute-start(bf16[4,128,256]{2,1,0:T(8,128)(2,1)S(1)} %get-tuple-element.47), channel_id=1, source_target_pairs={{0,4},{1,5},{2,6},{3,7},{4,0},{5,1},{6,2},{7,3},{8,12},{9,13},{10,... | collective-permute-start | bytes 786440 | tf_op jit(solution)/shard_map/ppermute | solution.py:192
  37.3 12.5 %collective-permute-start.11 = (bf16[4,128,256]{2,1,0:T(8,128)(2,1)S(1)}, bf16[4,128,256]{2,1,0:T(8,128)(2,1)S(1)}, u32[]{:S(2)}, u32[]{:S(2)}) collective-permute-start(bf16[4,128,256]{2,1,0:T(8,128)(2,1)S(1)} %get-tuple-element.48), channel_id=1, source_target_pairs={{0,252},{1,253},{2,254},{3,255},{4,8},{5,9},{6,10},{7,11},{8,4},{9... | collective-permute-start | bytes 786440 | tf_op jit(solution)/shard_map/ppermute | solution.py:192
  52.6 1.3 %collective-permute-start.12 = (f32[8,256]{1,0:T(8,128)S(1)}, f32[8,256]{1,0:T(8,128)S(1)}, u32[]{:S(2)}, u32[]{:S(2)}) collective-permute-start(f32[8,256]{1,0:T(8,128)S(1)} %get-tuple-element.51.own), channel_id=1, source_target_pairs={{0,4},{4,0},{1,5},{5,1},{2,6},{6,2},{3,7},{7,3},{8,12},{12,8},{9,1... | collective-permute-start | bytes 24584 | tf_op jit(solution)/shard_map/ppermute | solution.py:287
